TPU v7x, 32 devices: a whole 2x2x4 slice. The times are simulated.
32 devices in a mesh: dp: 4 (over x, core), tensor: 8 (over z, y).
Axes of the slice: x: 2, y: 2, z: 4, core: 2. Of those that a mesh axis runs over, the one named last changes fastest.
Arguments:
- grad_out: bfloat16 [256, 4096], P(('dp', 'tensor')), may hold values from -6 to 6
- gate_pre: bfloat16 [256, 14848], P('dp', 'tensor'), may hold values from -8 to 8
- up_pre: bfloat16 [256, 14848], P('dp', 'tensor'), may hold values from -6 to 6
- down_weight: bfloat16 [4096, 14848], P(None, 'tensor'), may hold values from -1.5 to 1.5
Outputs:
- grad_weight: float32 [4096, 14848], P('dp', 'tensor')
- grad_gate: bfloat16 [256, 14848], P('dp', 'tensor')
- grad_up: bfloat16 [256, 14848], P('dp', 'tensor')
All inputs are finite; a program needn't handle non-finite values.
Results may differ from a plain program's by a relative error of at most 0.015.
Values may be sent and summed in bfloat16 or wider, within the bound.
A program may use at most 128 MiB of HBM per device.

v0:
```python
import jax
import jax.numpy as jnp
from jax import lax
from jax.sharding import PartitionSpec as P


def contract_rows(left, right):
    return lax.dot_general(
        left, right, (((0,), (0,)), ((), ())), preferred_element_type=jnp.float32
    )


def body(grad_out, gate_pre, up_pre, down_weight):
    gate = gate_pre.astype(jnp.float32)
    upper = up_pre.astype(jnp.float32)
    sig = jax.nn.sigmoid(gate)
    act = gate * sig
    hidden = (act * upper).astype(jnp.bfloat16)
    whole = lax.all_gather(grad_out, "tensor", axis=0, tiled=True)
    grad_hidden = jnp.dot(whole, down_weight, preferred_element_type=jnp.float32)
    grad_weight = lax.psum_scatter(
        contract_rows(whole, hidden).astype(jnp.bfloat16), "dp", scatter_dimension=0, tiled=True
    ).astype(jnp.float32)
    grad_up = (grad_hidden * act).astype(jnp.bfloat16)
    grad_gate = (grad_hidden * upper * sig * (1.0 + gate * (1.0 - sig))).astype(jnp.bfloat16)
    return (grad_weight, grad_gate, grad_up)


def solution(mesh):
    in_specs = (P(("dp", "tensor"), None), P("dp", "tensor"), P("dp", "tensor"), P(None, "tensor"))
    out_specs = (P("dp", "tensor"), P("dp", "tensor"), P("dp", "tensor"))
    return jax.shard_map(body, mesh=mesh, in_specs=in_specs, out_specs=out_specs, check_vma=False)
```

profile of v0, /device:TPU:0, one launch (start us, length us, event | category | flops | bytes accessed | tf_op | source)
XLA Modules:
  0.0 176.6 jit_solution(7951081600380238514)
XLA Ops:
  7.2 0.0 reduce-scatter.2.cloned.1.call-start
  7.2 33.2 %all_gather.3 = bf16[64,4096]{1,0:T(8,128)(2,1)S(1)} all-gather(bf16[8,4096]{1,0:T(8,128)(2,1)} %param.4), channel_id=1, replica_groups=mesh['dp'=4,'tensor'=8] {'tensor'}, dimensions={0}, use_global_device_ids=true | all-gather | bytes 589824 | tf_op jit(solution)/shard_map/all_gather | solution.py:19
  40.5 0.0 copy-start
  40.5 0.0 copy-start.1
  40.5 8.6 %convert_bitcast_fusion = bf16[4096,1856]{0,1:T(8,128)(2,1)} fusion(bf16[64,4096]{1,0:T(8,128)(2,1)S(1)} %all_gather.3, bf16[64,1856]{1,0:T(8,128)(2,1)} %param.6, bf16[64,1856]{1,0:T(8,128)(2,1)} %param.5), kind=kOutput, calls=%fused_computation | convolution fusion | flops 981630976 | bytes 16203776 | tf_op jit(solution)/shard_map/dot_general | solution.py:8
  49.0 0.0 reduce-scatter.2.cloned.1.call-update
  49.1 0.0 copy-done
  49.1 0.0 copy-done.1
  49.1 10.8 %multiply_convert_fusion = (bf16[64,1856]{1,0:T(8,128)(2,1)}, bf16[64,1856]{1,0:T(8,128)(2,1)}) fusion(bf16[64,1856]{1,0:T(8,128)(2,1)S(1)} %copy-done.1, bf16[64,1856]{1,0:T(8,128)(2,1)S(1)} %copy-done, bf16[64,4096]{1,0:T(8,128)(2,1)S(1)} %all_gather.3, bf16[4096,1856]{0,1:T(8,128)(2,1)} %param.7), kind=kOutput, calls=%fused_computation.14 | convolution fusion | flops 974860288 | bytes 16678912 | tf_op jit(solution)/shard_map/dot_general | solution.py:20
  59.9 103.7 %reduce-scatter.2.cloned.1.call-done = bf16[1024,1856]{0,1:T(8,128)(2,1)} async-done(((bf16[4096,1856]{0,1:T(8,128)(2,1)}), bf16[1024,1856]{0,1:T(8,128)(2,1)}) %reduce-scatter.2.cloned.1.call-update) | async-done | bytes 3801104 | tf_op jit(solution)/shard_map/reduce_scatter | solution.py:21
  163.6 6.1 %convert_element_type.29 = f32[1024,1856]{0,1:T(8,128)} convert(bf16[1024,1856]{0,1:T(8,128)(2,1)} %reduce-scatter.2.cloned.1.call-done) | non-fusion elementwise | flops 1900544 | bytes 11403264 | tf_op jit(solution)/shard_map/convert_element_type | solution.py:23
Async XLA Ops:
  7.2 156.5 %reduce-scatter.2.cloned.1.call-start = ((), (), s32[]{:S(2)}) async-start(), calls=%async_computation.1 | async-start | bytes 19005440 | tf_op jit(solution)/shard_map/reduce_scatter | solution.py:21
  40.5 8.6 %copy-start = (bf16[64,1856]{1,0:T(8,128)(2,1)S(1)}, bf16[64,1856]{1,0:T(8,128)(2,1)}, u32[]{:S(2)}) copy-start(bf16[64,1856]{1,0:T(8,128)(2,1)} %param.6) | copy-start | bytes 712708
  40.5 8.6 %copy-start.1 = (bf16[64,1856]{1,0:T(8,128)(2,1)S(1)}, bf16[64,1856]{1,0:T(8,128)(2,1)}, u32[]{:S(2)}) copy-start(bf16[64,1856]{1,0:T(8,128)(2,1)} %param.5) | copy-start | bytes 712708
Sparse Core Ops, SparseCore 0:
  49.2 114.3 reduce-scatter.1
where the time goes:
time: 177 us
  waiting for transfers between devices  104 us (59%)
  blocking collectives  33.2 us (19%)
  matrix products  19.4 us (11%)
  between operations  14 us (8%)
  other arithmetic  6.15 us (3%)
    reduce_scatter x1, waiting for transfers between devices, body(): lax.psum_scatter(contract_rows(whole, hidden).astype(jnp.bfloat16), 'dp',...  104 us
    all_gather x1, blocking collectives, body(): whole = lax.all_gather(grad_out, 'tensor', axis=0, tiled=True)  33.2 us
    dot_general x1, matrix products, body(): jnp.dot(whole, down_weight, preferred_element_type=jnp.float32)  10.8 us
    dot_general x1, matrix products, contract_rows(): lax.dot_general(left, right, (((0,), (0,)), ((), ())), preferred_element_...  8.57 us
    convert_element_type x1, other arithmetic, body(): grad_weight = lax.psum_scatter(contract_rows(whole, hidden).astype(jnp.bf...  6.15 us
  transfers between devices with their start and end apart: 1, of which 1 were waited for; matrix products, arithmetic and copies ran while one was open for 6% of the time, Pallas kernels for 0%

commit v1 on v0

v1 whole, which is shorter than its diff:
```python
import functools

import jax
import jax.numpy as jnp
from jax import lax
from jax.experimental import pallas as pl
from jax.experimental.pallas import tpu as pltpu
from jax.sharding import PartitionSpec as P

MESH = pl.DeviceIdType.MESH
CORES = 2


def gather_kernel(
    n_dp, n_t, outer, widths,
    go_hbm, gate_hbm, up_hbm, weight_hbm,
    cols_ref, hidden_ref, grad_ref,
    rows, gate, upper, weight, left,
    load_sem, weight_sem, send_sem,
    rows_sem, cross_sem, line_sem, hidden_sem, pair_sem,
):
    inner = n_t // outer
    n_chip = n_dp // CORES
    depth = go_hbm.shape[0]
    feats = cols_ref.shape[-1]
    dp, t = lax.axis_index("dp"), lax.axis_index("tensor")
    chip, core = dp // CORES, dp % CORES
    mate = chip * CORES + (1 - core)
    a, b = t // inner, t % inner
    chips = [lax.rem(chip + d, n_chip) for d in range(1, n_chip)]
    lines = [lax.rem(a + d, outer) * inner + b for d in range(1, outer)]
    sides = [a * inner + lax.rem(b + d, inner) for d in range(1, inner)]

    loads = [
        pltpu.make_async_copy(go_hbm, rows.at[t], load_sem.at[0]),
        pltpu.make_async_copy(gate_hbm, gate, load_sem.at[1]),
        pltpu.make_async_copy(up_hbm, upper, load_sem.at[2]),
    ]
    for load in loads:
        load.start()
    weight_loads = []
    start = 0
    for k, width in enumerate(widths):
        span = pl.ds(start, width)
        weight_loads.append(pltpu.make_async_copy(weight_hbm.at[:, span], weight.at[:, span], weight_sem.at[k]))
        weight_loads[-1].start()
        start += width

    barrier = pltpu.get_barrier_semaphore()
    peers = [(lax.rem(dp + d, n_dp), t) for d in range(1, n_dp)]
    peers += [(dp, other) for other in lines + sides]
    for peer in peers:
        pl.semaphore_signal(barrier, inc=1, device_id=peer, device_id_type=MESH)
    loads[0].wait()
    pl.semaphore_wait(barrier, len(peers))

    sent = []

    def send(src, dst, sem, peer):
        copy = pltpu.make_async_remote_copy(
            src_ref=src, dst_ref=dst, send_sem=send_sem.at[len(sent)], recv_sem=sem,
            device_id=peer, device_id_type=MESH,
        )
        copy.start()
        sent.append(copy)

    def arrived(dst, sem):
        pltpu.make_async_remote_copy(
            src_ref=dst, dst_ref=dst, send_sem=send_sem.at[0], recv_sem=sem,
            device_id=(mate, t), device_id_type=MESH,
        ).wait_recv()

    def block_of(group):
        return pl.ds(pl.multiple_of(group * feats, feats), feats)

    for other in chips:
        for c in range(CORES):
            group = other * CORES + c
            send(rows.at[t, :, block_of(group)], cols_ref.at[chip, core, t], cross_sem.at[chip, core], (group, t))
    for peer in lines + sides:
        send(rows.at[t], rows.at[t], rows_sem.at[t], (dp, peer))

    loads[1].wait()
    loads[2].wait()
    g = gate[...].astype(jnp.float32)
    u = upper[...].astype(jnp.float32)
    hidden_ref[chip, core] = (g * jax.nn.sigmoid(g) * u).astype(jnp.bfloat16)
    mine = hidden_ref.at[chip, core]
    for other in chips:
        send(mine, mine, hidden_sem.at[chip, core], (other * CORES + core, t))
    send(mine, mine, hidden_sem.at[chip, core], (mate, t))

    for other in chips:
        for c in range(CORES):
            arrived(cols_ref.at[other, c, t], cross_sem.at[other, c])
        block = cols_ref.at[other, :, t]
        for peer in lines + sides:
            send(block, block, line_sem.at[other, t], (dp, peer))

    for source in lines:
        arrived(rows.at[source], rows_sem.at[source])
        for side in sides:
            send(rows.at[source], rows.at[source], rows_sem.at[source], (dp, side))
    for source in lines:
        for other in chips:
            block = cols_ref.at[other, :, source]
            arrived(block, line_sem.at[other, source])
            for side in sides:
                send(block, block, line_sem.at[other, source], (dp, side))

    for other in chips:
        block = hidden_ref.at[other, core]
        arrived(block, hidden_sem.at[other, core])
        send(block, block, hidden_sem.at[other, core], (mate, t))

    from_sides = [
        step * inner + lax.rem(b + d, inner)
        for step in range(outer) for d in range(1, inner)
    ]
    for source in from_sides:
        arrived(rows.at[source], rows_sem.at[source])
    send(rows.at[:, :, block_of(mate)], cols_ref.at[chip, core], pair_sem.at[0], (mate, t))
    keep = pltpu.make_async_copy(rows.at[:, :, block_of(dp)], cols_ref.at[chip, core], load_sem.at[3])
    keep.start()

    left[...] = rows[...].astype(jnp.float32).reshape(n_t * depth, -1).astype(jnp.bfloat16)
    start = 0
    for k, width in enumerate(widths):
        weight_loads[k].wait()
        span = pl.ds(start, width)
        grad_ref[:, span] = jnp.dot(left[...], weight[:, span], preferred_element_type=jnp.float32)
        start += width

    for source in from_sides:
        for other in chips:
            arrived(cols_ref.at[other, :, source], line_sem.at[other, source])
    for other in chips + [chip]:
        arrived(hidden_ref.at[other, 1 - core], hidden_sem.at[other, 1 - core])
    arrived(cols_ref.at[chip, 1 - core], pair_sem.at[0])
    keep.wait()
    for copy in sent:
        copy.wait_send()


def finish_kernel(cols_ref, hidden_ref, grad_ref, gate_ref, up_ref, weight_out, gate_out, up_out):
    weight_out[...] = lax.dot_general(
        cols_ref[...], hidden_ref[...], (((0,), (0,)), ((), ())), preferred_element_type=jnp.float32
    )
    grad = grad_ref[...]
    gate = gate_ref[...].astype(jnp.float32)
    upper = up_ref[...].astype(jnp.float32)
    sig = jax.nn.sigmoid(gate)
    up_out[...] = (grad * (gate * sig)).astype(jnp.bfloat16)
    gate_out[...] = (grad * upper * sig * (1.0 + gate * (1.0 - sig))).astype(jnp.bfloat16)


def body(n_dp, n_t, grad_out, gate_pre, up_pre, down_weight):
    depth, model = grad_out.shape
    group, wide = gate_pre.shape
    feats = model // n_dp
    n_chip = n_dp // CORES
    outer = 4 if n_t % 4 == 0 else 1
    inner = n_t // outer
    step = 512
    widths = [min(step, wide - start) for start in range(0, wide, step)]
    n_send = (
        (n_chip - 1) * CORES + (outer + inner - 2) * n_chip + n_chip
        + (outer - 1) * (inner - 1) * n_chip + n_chip + 1
    )
    anywhere = pl.BlockSpec(memory_space=pl.ANY)
    vmem = pl.BlockSpec(memory_space=pltpu.VMEM)
    dma = pltpu.SemaphoreType.DMA
    cols, hidden, grad = pl.pallas_call(
        functools.partial(gather_kernel, n_dp, n_t, outer, widths),
        out_shape=[
            jax.ShapeDtypeStruct((n_chip, CORES, n_t, depth, feats), jnp.bfloat16),
            jax.ShapeDtypeStruct((n_chip, CORES, group, wide), jnp.bfloat16),
            jax.ShapeDtypeStruct((group, wide), jnp.float32),
        ],
        in_specs=[anywhere] * 4,
        out_specs=[vmem] * 3,
        scratch_shapes=[
            pltpu.VMEM((n_t, depth, model), jnp.bfloat16),
            pltpu.VMEM((group, wide), jnp.bfloat16),
            pltpu.VMEM((group, wide), jnp.bfloat16),
            pltpu.VMEM((model, wide), jnp.bfloat16),
            pltpu.VMEM((group, model), jnp.bfloat16),
            dma((4,)),
            dma((len(widths),)),
            dma((n_send,)),
            dma((n_t,)),
            dma((n_chip, CORES)),
            dma((n_chip, n_t)),
            dma((n_chip, CORES)),
            dma((1,)),
        ],
        compiler_params=pltpu.CompilerParams(
            collective_id=0, has_side_effects=True, vmem_limit_bytes=48 * 1024 * 1024
        ),
    )(grad_out, gate_pre, up_pre, down_weight)
    cols = cols.reshape(n_dp * group, feats)
    hidden = hidden.reshape(n_dp * group, wide)

    tile = 128 if feats % 128 == 0 else feats
    steps = feats // tile
    while group % (steps * 16) != 0:
        tile, steps = tile * 2, steps // 2
    part = group // steps
    rows = pl.BlockSpec((part, wide), lambda i: (i, 0))
    return pl.pallas_call(
        finish_kernel,
        grid=(steps,),
        out_shape=[
            jax.ShapeDtypeStruct((feats, wide), jnp.float32),
            jax.ShapeDtypeStruct((group, wide), jnp.bfloat16),
            jax.ShapeDtypeStruct((group, wide), jnp.bfloat16),
        ],
        in_specs=[
            pl.BlockSpec((n_dp * group, tile), lambda i: (0, i)),
            pl.BlockSpec((n_dp * group, wide), lambda i: (0, 0)),
            rows, rows, rows,
        ],
        out_specs=[pl.BlockSpec((tile, wide), lambda i: (i, 0)), rows, rows],
        compiler_params=pltpu.CompilerParams(vmem_limit_bytes=48 * 1024 * 1024),
    )(cols, hidden, grad, gate_pre, up_pre)


def solution(mesh):
    in_specs = (P(("dp", "tensor"), None), P("dp", "tensor"), P("dp", "tensor"), P(None, "tensor"))
    out_specs = (P("dp", "tensor"), P("dp", "tensor"), P("dp", "tensor"))
    fn = functools.partial(body, mesh.shape["dp"], mesh.shape["tensor"])
    return jax.shard_map(fn, mesh=mesh, in_specs=in_specs, out_specs=out_specs, check_vma=False)
```

time: 177 us -> 56 us (0.32)
  waiting for transfers between devices: 104 us -> 0 us
  blocking collectives: 33.2 us -> 0 us
  local copies, waits for them, and re-layouts: 0.01 us -> 28.1 us
  Pallas kernels: 0 us -> 26.4 us
  matrix products: 19.4 us -> 0 us
  between operations: 14 us -> 0.67 us
  other arithmetic: 6.15 us -> 0 us
    reduce_scatter x1 -> x0, waiting for transfers between devices: 104 us -> none  [body(): lax.psum_scatter(contract_rows(whole, hidden).astype(jnp.bfloat16), 'dp',...]
    all_gather x1 -> x0, blocking collectives: 33.2 us -> none  [body(): whole = lax.all_gather(grad_out, 'tensor', axis=0, tiled=True)]
    pallas_call x0 -> x2, Pallas kernels: none -> 26.4 us  [the longest x1 22.1 us: body(): pl.pallas_call(functools.partial(gather_kernel, n_dp, n_t, outer, widths)...]
    dot_general x2 -> x0, matrix products: 19.4 us -> none  [the longest x1 10.8 us: body(): jnp.dot(whole, down_weight, preferred_element_type=jnp.float32)]
    unnamed x4 -> x7, local copies, waits for them, and re-layouts: 0.01 us -> 19.2 us
    pallas_call x0 -> x1, local copies, waits for them, and re-layouts: none -> 8.98 us  [body(): pl.pallas_call(finish_kernel, grid=(steps,), out_shape=[jax.ShapeDtypeStr...]
    convert_element_type x1 -> x0, other arithmetic: 6.15 us -> none  [body(): grad_weight = lax.psum_scatter(contract_rows(whole, hidden).astype(jnp.bf...]
  transfers between devices with their start and end apart: 1 -> 0, of which waited for: 1 -> 0; matrix products, arithmetic and copies ran while one was open for 6% -> 0% of each run, Pallas kernels for 0% -> 0%
where the time goes in v1:
time: 56 us; the launch traced here: 55.2 us
  local copies, waits for them, and re-layouts  28.1 us (50%)
  Pallas kernels  26.4 us (47%)
  between operations  0.67 us (1%)
    pallas_call x1, Pallas kernels, body(): pl.pallas_call(functools.partial(gather_kernel, n_dp, n_t, outer, widths)...  22.1 us
    unnamed x7, local copies, waits for them, and re-layouts  19.2 us
    pallas_call x1, local copies, waits for them, and re-layouts, body(): pl.pallas_call(finish_kernel, grid=(steps,), out_shape=[jax.ShapeDtypeStr...  8.98 us
    pallas_call x1, Pallas kernels, body(): pl.pallas_call(finish_kernel, grid=(steps,), out_shape=[jax.ShapeDtypeStr...  4.28 us

profile of v1, /device:TPU:0, one launch (start us, length us, event | category | flops | bytes accessed | tf_op | source)
XLA Modules:
  0.0 55.2 jit_solution(16315933295629494955)
XLA Ops:
  0.6 0.0 copy-start.1
  0.6 0.0 copy-start
  0.7 0.0 copy-start.2
  0.7 19.2 %copy.7.weight_hbm = bf16[4096,1856]{1,0:T(8,128)(2,1)} copy(bf16[4096,1856]{0,1:T(8,128)(2,1)} %param.7) | data formatting | bytes 30408704 | tf_op args[3]
  19.8 0.0 copy-done.1
  19.8 0.0 copy-done
  19.8 0.0 copy-done.2
  19.8 22.1 %shard_map.67 = (bf16[2,2,8,8,1024]{4,3,2,1,0:T(8,128)(2,1)S(1)}, bf16[2,2,64,1856]{3,2,1,0:T(8,128)(2,1)S(1)}, f32[64,1856]{1,0:T(8,128)S(1)}) custom-call(bf16[8,4096]{1,0:T(8,128)(2,1)S(1)} %copy-done.2, bf16[64,1856]{1,0:T(8,128)(2,1)S(1)} %copy-done, bf16[64,1856]{1,0:T(8,128)(2,1)S(1)} %copy-done.1, bf16[4096,1856]{1,0:T(8,128)(2,1)} %copy.7.weight_hbm), custom_call_target="tpu_custom_call" | custom-call | tf_op jit(solution)/shard_map/pallas_call | solution.py:173
  41.9 4.3 %shard_map.68 = (f32[1024,1856]{1,0:T(8,128)}, bf16[64,1856]{1,0:T(8,128)(2,1)}, bf16[64,1856]{1,0:T(8,128)(2,1)}) custom-call(bf16[256,1024]{1,0:T(8,128)(2,1)S(1)} %bitcast.3, bf16[256,1856]{1,0:T(8,128)(2,1)S(1)} %bitcast.2, f32[64,1856]{1,0:T(8,128)S(1)} %get-tuple-element.8.grad_ref, bf16[64,1856]{1,0:T(8,128)(2,1)S(1)} %copy-done, ...), custom_call_target="tpu_custom_call" | custom-call | tf_op jit(solution)/shard_map/pallas_call | solution.py:210
  46.2 9.0 %copy.8 = f32[1024,1856]{0,1:T(8,128)} copy(f32[1024,1856]{1,0:T(8,128)} %get-tuple-element.9) | data formatting | bytes 15204352 | tf_op jit(solution)/shard_map/pallas_call | solution.py:210
Async XLA Ops:
  0.6 19.2 %copy-start.1 = (bf16[64,1856]{1,0:T(8,128)(2,1)S(1)}, bf16[64,1856]{1,0:T(8,128)(2,1)}, u32[]{:S(2)}) copy-start(bf16[64,1856]{1,0:T(8,128)(2,1)} %up_ref.1) | copy-start | bytes 712708
  0.6 19.2 %copy-start = (bf16[64,1856]{1,0:T(8,128)(2,1)S(1)}, bf16[64,1856]{1,0:T(8,128)(2,1)}, u32[]{:S(2)}) copy-start(bf16[64,1856]{1,0:T(8,128)(2,1)} %gate_ref.1) | copy-start | bytes 712708
  0.7 19.2 %copy-start.2 = (bf16[8,4096]{1,0:T(8,128)(2,1)S(1)}, bf16[8,4096]{1,0:T(8,128)(2,1)}, u32[]{:S(2)}) copy-start(bf16[8,4096]{1,0:T(8,128)(2,1)} %go_hbm.1) | copy-start | bytes 196612

commit v2 on v1

--- a/solution.py
+++ b/solution.py
@@ -42,7 +42,7 @@
     start = 0
     for k, width in enumerate(widths):
         span = pl.ds(start, width)
-        weight_loads.append(pltpu.make_async_copy(weight_hbm.at[:, span], weight.at[:, span], weight_sem.at[k]))
+        weight_loads.append(pltpu.make_async_copy(weight_hbm.at[span], weight.at[span], weight_sem.at[k]))
         weight_loads[-1].start()
         start += width
 
@@ -128,7 +128,9 @@
     for k, width in enumerate(widths):
         weight_loads[k].wait()
         span = pl.ds(start, width)
-        grad_ref[:, span] = jnp.dot(left[...], weight[:, span], preferred_element_type=jnp.float32)
+        grad_ref[:, span] = lax.dot_general(
+            left[...], weight[span, :], (((1,), (1,)), ((), ())), preferred_element_type=jnp.float32
+        )
         start += width
 
     for source in from_sides:
@@ -144,7 +146,7 @@
 
 def finish_kernel(cols_ref, hidden_ref, grad_ref, gate_ref, up_ref, weight_out, gate_out, up_out):
     weight_out[...] = lax.dot_general(
-        cols_ref[...], hidden_ref[...], (((0,), (0,)), ((), ())), preferred_element_type=jnp.float32
+        hidden_ref[...], cols_ref[...], (((0,), (0,)), ((), ())), preferred_element_type=jnp.float32
     )
     grad = grad_ref[...]
     gate = gate_ref[...].astype(jnp.float32)
@@ -183,7 +185,7 @@
             pltpu.VMEM((n_t, depth, model), jnp.bfloat16),
             pltpu.VMEM((group, wide), jnp.bfloat16),
             pltpu.VMEM((group, wide), jnp.bfloat16),
-            pltpu.VMEM((model, wide), jnp.bfloat16),
+            pltpu.VMEM((wide, model), jnp.bfloat16),
             pltpu.VMEM((group, model), jnp.bfloat16),
             dma((4,)),
             dma((len(widths),)),
@@ -197,32 +199,29 @@
         compiler_params=pltpu.CompilerParams(
             collective_id=0, has_side_effects=True, vmem_limit_bytes=48 * 1024 * 1024
         ),
-    )(grad_out, gate_pre, up_pre, down_weight)
+    )(grad_out, gate_pre, up_pre, down_weight.T)
     cols = cols.reshape(n_dp * group, feats)
     hidden = hidden.reshape(n_dp * group, wide)
 
-    tile = 128 if feats % 128 == 0 else feats
-    steps = feats // tile
-    while group % (steps * 16) != 0:
-        tile, steps = tile * 2, steps // 2
-    part = group // steps
-    rows = pl.BlockSpec((part, wide), lambda i: (i, 0))
-    return pl.pallas_call(
+    tile = 256
+    tiles = pl.BlockSpec((group, tile), lambda i: (0, i))
+    turned, grad_gate, grad_up = pl.pallas_call(
         finish_kernel,
-        grid=(steps,),
+        grid=(pl.cdiv(wide, tile),),
         out_shape=[
-            jax.ShapeDtypeStruct((feats, wide), jnp.float32),
+            jax.ShapeDtypeStruct((wide, feats), jnp.float32),
             jax.ShapeDtypeStruct((group, wide), jnp.bfloat16),
             jax.ShapeDtypeStruct((group, wide), jnp.bfloat16),
         ],
         in_specs=[
+            pl.BlockSpec((n_dp * group, feats), lambda i: (0, 0)),
             pl.BlockSpec((n_dp * group, tile), lambda i: (0, i)),
-            pl.BlockSpec((n_dp * group, wide), lambda i: (0, 0)),
-            rows, rows, rows,
-        ],
-        out_specs=[pl.BlockSpec((tile, wide), lambda i: (i, 0)), rows, rows],
+            tiles, tiles, tiles,
+        ],
+        out_specs=[pl.BlockSpec((tile, feats), lambda i: (i, 0)), tiles, tiles],
         compiler_params=pltpu.CompilerParams(vmem_limit_bytes=48 * 1024 * 1024),
     )(cols, hidden, grad, gate_pre, up_pre)
+    return turned.T, grad_gate, grad_up
 
 
 def solution(mesh):

time: 56 us -> 34.2 us (0.61)
  local copies, waits for them, and re-layouts: 28.1 us -> 2.73 us
  Pallas kernels: 26.4 us -> 30.4 us
    unnamed x7 -> x10, local copies, waits for them, and re-layouts: 19.2 us -> 2.73 us
    pallas_call x1 -> x0, local copies, waits for them, and re-layouts: 8.98 us -> none  [body(): pl.pallas_call(finish_kernel, grid=(steps,), out_shape=[jax.ShapeDtypeStr...]
    pallas_call x1, Pallas kernels: 22.1 us -> 24.4 us  [body(): pl.pallas_call(functools.partial(gather_kernel, n_dp, n_t, outer, widths)...]
    pallas_call x1, Pallas kernels: 4.28 us -> 5.98 us  [body(): pl.pallas_call(finish_kernel, grid=(pl.cdiv(wide, tile),), out_shape=[jax...]
where the time goes in v2:
time: 34.2 us; the launch traced here: 33.8 us
  Pallas kernels  30.4 us (89%)
  local copies, waits for them, and re-layouts  2.73 us (8%)
  between operations  0.67 us (2%)
    pallas_call x1, Pallas kernels, body(): pl.pallas_call(functools.partial(gather_kernel, n_dp, n_t, outer, widths)...  24.4 us
    pallas_call x1, Pallas kernels, body(): pl.pallas_call(finish_kernel, grid=(pl.cdiv(wide, tile),), out_shape=[jax...  5.98 us
    unnamed x10, local copies, waits for them, and re-layouts  2.73 us

profile of v2, /device:TPU:0, one launch (start us, length us, event | category | flops | bytes accessed | tf_op | source)
XLA Modules:
  0.0 33.8 jit_solution(3210944535530060200)
XLA Ops:
  0.6 0.0 copy-start
  0.6 0.9 %copy-done = bf16[64,1856]{1,0:T(8,128)(2,1)S(1)} copy-done((bf16[64,1856]{1,0:T(8,128)(2,1)S(1)}, bf16[64,1856]{1,0:T(8,128)(2,1)}, u32[]{:S(2)}) %copy-start) | copy-done | bytes 237592
  1.6 0.0 copy-start.2
  1.6 0.9 %copy-done.2 = bf16[64,1856]{1,0:T(8,128)(2,1)S(1)} copy-done((bf16[64,1856]{1,0:T(8,128)(2,1)S(1)}, bf16[64,1856]{1,0:T(8,128)(2,1)}, u32[]{:S(2)}) %copy-start.2) | copy-done | bytes 237592
  2.5 0.0 copy-start.4
  2.5 0.8 %copy-done.4 = bf16[8,4096]{1,0:T(8,128)(2,1)S(1)} copy-done((bf16[8,4096]{1,0:T(8,128)(2,1)S(1)}, bf16[8,4096]{1,0:T(8,128)(2,1)}, u32[]{:S(2)}) %copy-start.4) | copy-done | bytes 65560
  3.4 0.0 copy-start.1
  3.4 0.0 copy-start.3
  3.4 24.4 %shard_map.67 = (bf16[2,2,8,8,1024]{4,3,2,1,0:T(8,128)(2,1)S(1)}, bf16[2,2,64,1856]{3,2,1,0:T(8,128)(2,1)S(1)}, f32[64,1856]{1,0:T(8,128)S(1)}) custom-call(bf16[8,4096]{1,0:T(8,128)(2,1)S(1)} %copy-done.4, bf16[64,1856]{1,0:T(8,128)(2,1)S(1)} %copy-done, bf16[64,1856]{1,0:T(8,128)(2,1)S(1)} %copy-done.2, bf16[1856,4096]{1,0:T(8,128)(2,1)} %bitcast.6), custom_call_target="tpu_custom_call" | custom-call | tf_op jit(solution)/shard_map/pallas_call | solution.py:175
  27.8 0.0 copy-done.1
  27.8 0.0 copy-done.3
  27.8 6.0 %shard_map.68 = (f32[1856,1024]{1,0:T(8,128)}, bf16[64,1856]{1,0:T(8,128)(2,1)}, bf16[64,1856]{1,0:T(8,128)(2,1)}) custom-call(bf16[256,1024]{1,0:T(8,128)(2,1)S(1)} %bitcast.5, bf16[256,1856]{1,0:T(8,128)(2,1)S(1)} %bitcast.4, f32[64,1856]{1,0:T(8,128)S(1)} %get-tuple-element.11.grad_ref, bf16[64,1856]{1,0:T(8,128)(2,1)S(1)} %copy-done.1, ...), custom_call_target="tpu_custom_call" | custom-call | tf_op jit(solution)/shard_map/pallas_call | solution.py:208
Async XLA Ops:
  0.6 0.9 %copy-start = (bf16[64,1856]{1,0:T(8,128)(2,1)S(1)}, bf16[64,1856]{1,0:T(8,128)(2,1)}, u32[]{:S(2)}) copy-start(bf16[64,1856]{1,0:T(8,128)(2,1)} %gate_ref.1) | copy-start | bytes 712708
  1.6 0.9 %copy-start.2 = (bf16[64,1856]{1,0:T(8,128)(2,1)S(1)}, bf16[64,1856]{1,0:T(8,128)(2,1)}, u32[]{:S(2)}) copy-start(bf16[64,1856]{1,0:T(8,128)(2,1)} %up_ref.1) | copy-start | bytes 712708
  2.5 0.8 %copy-start.4 = (bf16[8,4096]{1,0:T(8,128)(2,1)S(1)}, bf16[8,4096]{1,0:T(8,128)(2,1)}, u32[]{:S(2)}) copy-start(bf16[8,4096]{1,0:T(8,128)(2,1)} %go_hbm.1) | copy-start | bytes 196612
  3.4 24.4 %copy-start.1 = (bf16[64,1856]{1,0:T(8,128)(2,1)S(1)}, bf16[64,1856]{1,0:T(8,128)(2,1)}, u32[]{:S(2)}) copy-start(bf16[64,1856]{1,0:T(8,128)(2,1)} %gate_ref.1) | copy-start | bytes 712708
  3.4 24.4 %copy-start.3 = (bf16[64,1856]{1,0:T(8,128)(2,1)S(1)}, bf16[64,1856]{1,0:T(8,128)(2,1)}, u32[]{:S(2)}) copy-start(bf16[64,1856]{1,0:T(8,128)(2,1)} %up_ref.1) | copy-start | bytes 712708

commit v3 on v2

--- a/solution.py
+++ b/solution.py
@@ -9,6 +9,8 @@
 
 MESH = pl.DeviceIdType.MESH
 CORES = 2
+PARTS = 2
+VMEM = 67043328
 
 
 def gather_kernel(
@@ -23,6 +25,8 @@
     n_chip = n_dp // CORES
     depth = go_hbm.shape[0]
     feats = cols_ref.shape[-1]
+    share = go_hbm.shape[1] // PARTS
+    parts = [pl.ds(h * share, share) for h in range(PARTS)]
     dp, t = lax.axis_index("dp"), lax.axis_index("tensor")
     chip, core = dp // CORES, dp % CORES
     mate = chip * CORES + (1 - core)
@@ -77,8 +81,10 @@
         for c in range(CORES):
             group = other * CORES + c
             send(rows.at[t, :, block_of(group)], cols_ref.at[chip, core, t], cross_sem.at[chip, core], (group, t))
-    for peer in lines + sides:
-        send(rows.at[t], rows.at[t], rows_sem.at[t], (dp, peer))
+    for h, part in enumerate(parts):
+        mine = rows.at[t, :, part]
+        for peer in lines + sides:
+            send(mine, mine, rows_sem.at[h, t], (dp, peer))
 
     loads[1].wait()
     loads[2].wait()
@@ -97,41 +103,52 @@
         for peer in lines + sides:
             send(block, block, line_sem.at[other, t], (dp, peer))
 
-    for source in lines:
-        arrived(rows.at[source], rows_sem.at[source])
-        for side in sides:
-            send(rows.at[source], rows.at[source], rows_sem.at[source], (dp, side))
-    for source in lines:
+    for h, part in enumerate(parts):
+        for source in lines:
+            block = rows.at[source, :, part]
+            arrived(block, rows_sem.at[h, source])
+            for side in sides:
+                send(block, block, rows_sem.at[h, source], (dp, side))
+
+    for other in chips:
+        block = hidden_ref.at[other, core]
+        arrived(block, hidden_sem.at[other, core])
+        send(block, block, hidden_sem.at[other, core], (mate, t))
+
+    def pass_on(source):
         for other in chips:
             block = cols_ref.at[other, :, source]
             arrived(block, line_sem.at[other, source])
             for side in sides:
                 send(block, block, line_sem.at[other, source], (dp, side))
 
-    for other in chips:
-        block = hidden_ref.at[other, core]
-        arrived(block, hidden_sem.at[other, core])
-        send(block, block, hidden_sem.at[other, core], (mate, t))
-
     from_sides = [
         step * inner + lax.rem(b + d, inner)
         for step in range(outer) for d in range(1, inner)
     ]
-    for source in from_sides:
-        arrived(rows.at[source], rows_sem.at[source])
-    send(rows.at[:, :, block_of(mate)], cols_ref.at[chip, core], pair_sem.at[0], (mate, t))
-    keep = pltpu.make_async_copy(rows.at[:, :, block_of(dp)], cols_ref.at[chip, core], load_sem.at[3])
-    keep.start()
-
-    left[...] = rows[...].astype(jnp.float32).reshape(n_t * depth, -1).astype(jnp.bfloat16)
-    start = 0
-    for k, width in enumerate(widths):
-        weight_loads[k].wait()
-        span = pl.ds(start, width)
-        grad_ref[:, span] = lax.dot_general(
-            left[...], weight[span, :], (((1,), (1,)), ((), ())), preferred_element_type=jnp.float32
-        )
-        start += width
+    waiting = list(lines)
+    for h, part in enumerate(parts):
+        for source in from_sides:
+            arrived(rows.at[source, :, part], rows_sem.at[h, source])
+        if h == PARTS - 1:
+            send(rows.at[:, :, block_of(mate)], cols_ref.at[chip, core], pair_sem.at[0], (mate, t))
+            keep = pltpu.make_async_copy(rows.at[:, :, block_of(dp)], cols_ref.at[chip, core], load_sem.at[3])
+            keep.start()
+        left[:, part] = rows[:, :, part].astype(jnp.float32).reshape(n_t * depth, share).astype(jnp.bfloat16)
+        start = 0
+        for k, width in enumerate(widths):
+            if h == 0:
+                weight_loads[k].wait()
+            span = pl.ds(start, width)
+            term = lax.dot_general(
+                left[:, part], weight[span, part], (((1,), (1,)), ((), ())), preferred_element_type=jnp.float32
+            )
+            grad_ref[:, span] = term if h == 0 else grad_ref[:, span] + term
+            start += width
+            if waiting:
+                pass_on(waiting.pop(0))
+    while waiting:
+        pass_on(waiting.pop(0))
 
     for source in from_sides:
         for other in chips:
@@ -166,10 +183,11 @@
     step = 512
     widths = [min(step, wide - start) for start in range(0, wide, step)]
     n_send = (
-        (n_chip - 1) * CORES + (outer + inner - 2) * n_chip + n_chip
-        + (outer - 1) * (inner - 1) * n_chip + n_chip + 1
+        (n_chip - 1) * CORES + (outer * inner - 1) * (n_chip - 1 + PARTS) + 2 * n_chip
     )
-    anywhere = pl.BlockSpec(memory_space=pl.ANY)
+    lanes = pl.cdiv(wide, 128) * 128
+    results = 2 * n_dp * group * (feats + lanes) + 4 * group * lanes
+    anywhere = pl.BlockSpec(memory_space=pltpu.HBM)
     vmem = pl.BlockSpec(memory_space=pltpu.VMEM)
     dma = pltpu.SemaphoreType.DMA
     cols, hidden, grad = pl.pallas_call(
@@ -190,20 +208,20 @@
             dma((4,)),
             dma((len(widths),)),
             dma((n_send,)),
-            dma((n_t,)),
+            dma((PARTS, n_t)),
             dma((n_chip, CORES)),
             dma((n_chip, n_t)),
             dma((n_chip, CORES)),
             dma((1,)),
         ],
         compiler_params=pltpu.CompilerParams(
-            collective_id=0, has_side_effects=True, vmem_limit_bytes=48 * 1024 * 1024
+            collective_id=0, has_side_effects=True, vmem_limit_bytes=VMEM - results - 16 * 1024
         ),
     )(grad_out, gate_pre, up_pre, down_weight.T)
     cols = cols.reshape(n_dp * group, feats)
     hidden = hidden.reshape(n_dp * group, wide)
 
-    tile = 256
+    tile = 512
     tiles = pl.BlockSpec((group, tile), lambda i: (0, i))
     turned, grad_gate, grad_up = pl.pallas_call(
         finish_kernel,
@@ -219,7 +237,7 @@
             tiles, tiles, tiles,
         ],
         out_specs=[pl.BlockSpec((tile, feats), lambda i: (i, 0)), tiles, tiles],
-        compiler_params=pltpu.CompilerParams(vmem_limit_bytes=48 * 1024 * 1024),
+        compiler_params=pltpu.CompilerParams(vmem_limit_bytes=VMEM - results - 16 * 1024),
     )(cols, hidden, grad, gate_pre, up_pre)
     return turned.T, grad_gate, grad_up
 

time: 34.2 us -> 30 us (0.88)
  local copies, waits for them, and re-layouts: 2.73 us -> 0 us
  Pallas kernels: 30.4 us -> 29.2 us
    unnamed x10 -> x0, local copies, waits for them, and re-layouts: 2.73 us -> none
    pallas_call x1, Pallas kernels: 24.4 us -> 23.1 us  [body(): pl.pallas_call(functools.partial(gather_kernel, n_dp, n_t, outer, widths)...]
where the time goes in v3:
time: 30 us; the launch traced here: 29.8 us
  Pallas kernels  29.2 us (97%)
  between operations  0.64 us (2%)
    pallas_call x1, Pallas kernels, body(): pl.pallas_call(functools.partial(gather_kernel, n_dp, n_t, outer, widths)...  23.1 us
    pallas_call x1, Pallas kernels, body(): pl.pallas_call(finish_kernel, grid=(pl.cdiv(wide, tile),), out_shape=[jax...  6.14 us

profile of v3, /device:TPU:0, one launch (start us, length us, event | category | flops | bytes accessed | tf_op | source)
XLA Modules:
  0.0 29.8 jit_solution(10601026288652876305)
XLA Ops:
  0.6 23.1 %shard_map.67 = (bf16[2,2,8,8,1024]{4,3,2,1,0:T(8,128)(2,1)}, bf16[2,2,64,1856]{3,2,1,0:T(8,128)(2,1)}, f32[64,1856]{1,0:T(8,128)}) custom-call(bf16[8,4096]{1,0:T(8,128)(2,1)} %go_hbm.1, bf16[64,1856]{1,0:T(8,128)(2,1)} %gate_ref.1, bf16[64,1856]{1,0:T(8,128)(2,1)} %up_ref.1, bf16[1856,4096]{1,0:T(8,128)(2,1)} %bitcast.4), custom_call_target="tpu_custom_call" | custom-call | tf_op jit(solution)/shard_map/pallas_call | solution.py:193
  23.7 6.1 %shard_map.68 = (f32[1856,1024]{1,0:T(8,128)}, bf16[64,1856]{1,0:T(8,128)(2,1)}, bf16[64,1856]{1,0:T(8,128)(2,1)}) custom-call(bf16[256,1024]{1,0:T(8,128)(2,1)} %bitcast.6, bf16[256,1856]{1,0:T(8,128)(2,1)} %bitcast.5, f32[64,1856]{1,0:T(8,128)} %get-tuple-element.11.grad_ref, bf16[64,1856]{1,0:T(8,128)(2,1)} %gate_ref.1, bf16[64,1856]{1,0:T(8,128)(2,1)} %up_ref.1), custom_call_target="tpu_custom_call" | custom-call | tf_op jit(solution)/shard_map/pallas_call | solution.py:226
